TPU v7x, 32 devices: a whole 2x2x4 slice. The times are simulated.
32 devices in a mesh: mem: 4 (over y, core), lat: 4 (over z), lon: 2 (over x).
Axes of the slice: x: 2, y: 2, z: 4, core: 2. Of those that a mesh axis runs over, the one named last changes fastest.
Arguments:
- fields: bfloat16 [4, 2, 96, 96, 512], P('mem', None, 'lat', 'lon'), may hold values from -6 to 6
- region: int32 [96, 96], P('lat', 'lon'), may hold values from 0 to 2
- gain_attn: float32 [512], replicated, may hold values from 0.1 to 1.9
- w_qkv: bfloat16 [512, 1536], P(None, ('mem', 'lat', 'lon')), may hold values from -1 to 1
- w_proj: bfloat16 [512, 512], P(None, ('mem', 'lat', 'lon')), may hold values from -0.25 to 0.25
- gain_mlp: float32 [512], replicated, may hold values from 0.1 to 1.9
- w_up: bfloat16 [512, 2048], P(None, ('mem', 'lat', 'lon')), may hold values from -0.25 to 0.25
- w_down: bfloat16 [2048, 512], P(None, ('mem', 'lat', 'lon')), may hold values from -0.125 to 0.125
Outputs:
- updated: bfloat16 [4, 2, 96, 96, 512], P('mem', None, 'lat', 'lon')
All inputs are finite; a program needn't handle non-finite values.
Results may differ from a plain program's by a relative error of at most 0.011.
Values may be sent and summed in bfloat16 or wider, within the bound.
A program may use at most 192 MiB of HBM per device.

v0:
```python
import jax
import jax.numpy as jnp
from jax import lax
from jax.sharding import PartitionSpec as P

HEADS = 16
HDIM = 32
WLAT = 6
WLON = 12
SH = 3
SL = 6
eps = 1e-05


def shifted_2(block, axis, distance):
    devices = range(lax.axis_size(axis))
    route = [((i - distance) % len(devices), i) for i in devices]
    return lax.ppermute(block, axis, route)


def layer_norm(values, gain_vec):
    values = values.astype(jnp.float32)
    average = jnp.mean(values, axis=-1, keepdims=True)
    centred = values - average
    variance = jnp.mean(centred * centred, axis=-1, keepdims=True)
    return (centred * lax.rsqrt(variance + eps) * gain_vec).astype(jnp.bfloat16)


def attend(qkv_all, region_ids, north_side, height):
    levels, row_count, col_count, width3 = qkv_all.shape
    width = width3 // 3
    band_count = row_count // height
    win_count = col_count // WLON
    win_tok = levels * height * WLON
    windowed = qkv_all.reshape(levels, band_count, height, win_count, WLON, width3)
    windowed = windowed.transpose(1, 3, 0, 2, 4, 5).reshape(
        band_count * win_count, win_tok, 3, HEADS, width // HEADS
    )
    ids_full = jnp.broadcast_to(region_ids[None], (levels, row_count, col_count))
    ids_full = ids_full.reshape(levels, band_count, height, win_count, WLON).transpose(
        1, 3, 0, 2, 4
    )
    ids_full = ids_full.reshape(band_count * win_count, win_tok)
    north_full = jnp.broadcast_to(north_side[None, :, None], (levels, row_count, col_count))
    north_full = north_full.reshape(levels, band_count, height, win_count, WLON).transpose(
        1, 3, 0, 2, 4
    )
    north_full = north_full.reshape(band_count * win_count, win_tok)
    scores = jnp.einsum(
        "wqhd,wkhd->whqk", windowed[:, :, 0], windowed[:, :, 1], preferred_element_type=jnp.float32
    )
    scores = scores * (1.0 / HDIM**0.5)
    allow = (ids_full[:, :, None] == ids_full[:, None, :]) & (
        north_full[:, :, None] == north_full[:, None, :]
    )
    scores = jnp.where(allow[:, None], scores, -1000000000.0)
    attn_probs = jax.nn.softmax(scores, axis=-1).astype(jnp.bfloat16)
    mixed_heads = jnp.einsum(
        "whqk,wkhd->wqhd", attn_probs, windowed[:, :, 2], preferred_element_type=jnp.float32
    )
    mixed_heads = mixed_heads.astype(jnp.bfloat16).reshape(
        band_count, win_count, levels, height, WLON, width
    )
    return mixed_heads.transpose(2, 0, 3, 1, 4, 5).reshape(levels, row_count, col_count, width)


def body(fields, region, gain_attn, w_qkv, w_proj, gain_mlp, w_up, w_down):
    member = fields[0]
    levels, clat, clon, width = member.shape
    normed = layer_norm(member, gain_attn)
    region_ids = region.astype(jnp.bfloat16)
    lat_pos = lax.axis_index("lat")
    nlat_all = clat * lax.axis_size("lat")
    row_ids = jnp.arange(clat, dtype=jnp.int32)
    north_side = (lat_pos * clat + SH + row_ids) % nlat_all < SH
    arrived, arrived_ids = shifted_2((normed[:, :SH], region_ids[:SH]), "lat", -1)
    lat_band = jnp.concatenate([normed[:, SH:], arrived], axis=1)
    band_ids = jnp.concatenate([region_ids[SH:], arrived_ids], axis=0)
    strip, strip_ids = shifted_2((lat_band[:, :, :SL], band_ids[:, :SL]), "lon", -1)
    shifted = jnp.concatenate([lat_band[:, :, SL:], strip], axis=2)
    shifted_ids = jnp.concatenate([band_ids[:, SL:], strip_ids], axis=1)
    tok_rows = shifted.reshape(-1, width)
    qkv_all = (
        jnp.dot(
            tok_rows,
            lax.all_gather(w_qkv, ("mem", "lat", "lon"), axis=1, tiled=True),
            preferred_element_type=jnp.float32,
        )
        .astype(jnp.bfloat16)
        .reshape(levels, clat, clon, 3 * width)
    )
    mixed_heads = attend(qkv_all, shifted_ids, north_side, WLAT)
    proj_tok_rows = mixed_heads.reshape(-1, width)
    attn_out = (
        jnp.dot(
            proj_tok_rows,
            lax.all_gather(w_proj, ("mem", "lat", "lon"), axis=1, tiled=True),
            preferred_element_type=jnp.float32,
        )
        .astype(jnp.bfloat16)
        .reshape(levels, clat, clon, width)
    )
    arrived_cols = shifted_2(attn_out[:, :, clon - SL :], "lon", 1)
    attn_out = jnp.concatenate([arrived_cols, attn_out[:, :, : clon - SL]], axis=2)
    arrived_rows = shifted_2(attn_out[:, clat - SH :], "lat", 1)
    attn_out = jnp.concatenate([arrived_rows, attn_out[:, : clat - SH]], axis=1)
    resid = (member.astype(jnp.float32) + attn_out.astype(jnp.float32)).astype(jnp.bfloat16)
    normed2 = layer_norm(resid, gain_mlp).reshape(-1, width)
    pre_act = jnp.dot(
        normed2,
        lax.all_gather(w_up, ("mem", "lat", "lon"), axis=1, tiled=True),
        preferred_element_type=jnp.float32,
    )
    hidden = jax.nn.gelu(pre_act, approximate=False).astype(jnp.bfloat16)
    delta = jnp.dot(
        hidden,
        lax.all_gather(w_down, ("mem", "lat", "lon"), axis=1, tiled=True),
        preferred_element_type=jnp.float32,
    ).reshape(levels, clat, clon, width)
    updated = (resid.astype(jnp.float32) + delta).astype(jnp.bfloat16)
    return updated[None]


def solution(mesh):
    in_specs = (
        P("mem", None, "lat", "lon", None),
        P("lat", "lon"),
        P(),
        P(None, ("mem", "lat", "lon")),
        P(None, ("mem", "lat", "lon")),
        P(),
        P(None, ("mem", "lat", "lon")),
        P(None, ("mem", "lat", "lon")),
    )
    out_specs = P("mem", None, "lat", "lon", None)
    return jax.shard_map(body, mesh=mesh, in_specs=in_specs, out_specs=out_specs, check_vma=False)
```

profile of v0, /device:TPU:0, one launch (start us, length us, event | category | flops | bytes accessed | tf_op | source)
XLA Modules:
  0.0 395.8 jit_solution(3137256965465653519)
XLA Ops:
  6.5 0.7 all-gather.4.cloned.1.call-update
  7.3 2.0 convert_reduce_fusion.1
  9.4 2.7 fusion.27
  12.1 0.9 fusion.29
  13.1 1.4 copy-done.5
  14.5 5.1 %collective-permute-start = (bf16[2,3,48,512]{3,2,1,0:T(8,128)(2,1)S(1)}, bf16[2,3,48,512]{3,2,1,0:T(8,128)(2,1)S(1)}, u32[]{:S(2)}, u32[]{:S(2)}) collective-permute-start(bf16[2,3,48,512]{3,2,1,0:T(8,128)(2,1)S(1)} %slice.61), channel_id=1, source_target_pairs={{2,0},{4,2},{6,4},{0,6},{3,1},{5,3},{7,5},{1,7},{10,8},{12,10},{14... | collective-permute-start | bytes 884744 | tf_op jit(solution)/shard_map/ppermute | solution.py:18
  19.7 0.5 collective-permute-start.2
  20.2 76.2 %all_gather.13 = bf16[512,512]{0,1:T(8,128)(2,1)} all-gather(bf16[512,16]{0,1:T(8,128)(2,1)S(1)} %copy-done.6), channel_id=1, replica_groups=mesh['mem'=4,'lat'=4,'lon'=2] {'mem','lat','lon'}, dimensions={1}, use_global_device_ids=true | all-gather | bytes 540672 | tf_op jit(solution)/shard_map/all_gather | solution.py:97
  96.5 1.8 slice.60
  98.3 0.1 transpose.33
  98.4 0.1 eq.44
  98.6 0.1 slice_maximum_fusion.1
  98.7 3.7 collective-permute-done.3
  102.4 0.1 pad_maximum_fusion.5
  102.5 0.1 broadcast_in_dim.12
  102.6 0.1 eq.40
  102.8 1.4 compare_and_fusion
  104.2 0.6 slice_maximum_fusion
  104.8 5.8 %collective-permute-done.1 = bf16[2,24,6,512]{3,2,1,0:T(8,128)(2,1)S(1)} collective-permute-done((bf16[2,24,6,512]{3,2,1,0:T(8,128)(2,1)S(1)}, bf16[2,24,6,512]{3,2,1,0:T(8,128)(2,1)S(1)}, u32[]{:S(2)}, u32[]{:S(2)}) %collective-permute-start.1) | collective-permute-done | bytes 294944 | tf_op jit(solution)/shard_map/ppermute | solution.py:18
  110.6 0.4 pad_maximum_fusion
  111.0 7.3 %convolution_convert_fusion = bf16[2304,1536]{1,0:T(8,128)(2,1)} fusion(bf16[2304,512]{1,0:T(8,128)(2,1)S(1)} %bitcast.91, bf16[512,1536]{0,1:T(8,128)(2,1)} %all-gather.4.cloned.1.call-done), kind=kOutput, calls=%fused_computation.29 | convolution fusion | flops 3627417600 | bytes 11010048 | tf_op jit(solution)/shard_map/dot_general | solution.py:84
  118.3 11.4 %reshape_reshape.6 = bf16[2,4,6,4,12,1536]{5,4,3,2,1,0:T(8,128)(2,1)} reshape(bf16[2304,1536]{1,0:T(8,128)(2,1)} %convolution_convert_fusion) | data formatting | bytes 14155776 | tf_op jit(solution)/shard_map/reshape;reshape | solution.py:35
  129.7 12.0 %copy.11 = bf16[4,4,2,6,12,1536]{5,1,0,4,3,2:T(4,128)(2,1)} copy(bf16[4,4,2,6,12,1536]{5,4,1,3,0,2:T(8,128)(2,1)} %bitcast.84) | data formatting | bytes 14155776 | tf_op jit(solution)/shard_map/transpose | solution.py:36
  141.6 32.5 %reshape.120 = bf16[16,144,3,16,32]{4,3,2,0,1:T(8,128)(2,1)} reshape(bf16[4,4,2,6,12,1536]{5,1,0,4,3,2:T(4,128)(2,1)} %copy.11) | data formatting | bytes 14155776 | tf_op jit(solution)/shard_map/reshape | solution.py:36
  174.1 24.0 %fusion.88 = (bf16[16,144,1,16,32]{4,3,2,0,1:T(8,128)(2,1)}, bf16[16,144,1,16,32]{4,3,2,0,1:T(8,128)(2,1)}, bf16[16,144,1,16,32]{4,3,2,0,1:T(8,128)(2,1)}) fusion(bf16[16,144,3,16,32]{4,3,2,0,1:T(8,128)(2,1)} %reshape.120), kind=kLoop, calls=%fused_computation.115 | loop fusion | bytes 14155776 | tf_op jit(solution)/shard_map/slice | solution.py:59
  198.1 12.3 %copy.21 = bf16[16,144,1,16,32]{1,4,3,0,2:T(8,128)(2,1)} copy(bf16[16,144,1,16,32]{4,3,2,0,1:T(8,128)(2,1)} %get-tuple-element.6) | data formatting | bytes 4718592
  210.4 12.4 %copy.22 = bf16[16,144,1,16,32]{1,4,3,0,2:T(8,128)(2,1)} copy(bf16[16,144,1,16,32]{4,3,2,0,1:T(8,128)(2,1)} %get-tuple-element.7) | data formatting | bytes 4718592
  222.8 12.3 %copy.20 = bf16[16,144,1,16,32]{1,4,3,0,2:T(8,128)(2,1)} copy(bf16[16,144,1,16,32]{4,3,2,0,1:T(8,128)(2,1)} %get-tuple-element.5) | data formatting | bytes 4718592
  235.1 19.9 %fusion.89 = (f32[16,16,144]{2,1,0:T(8,128)S(1)}, f32[16,16,144,144]{2,3,1,0:T(8,128)}) fusion(pred[16,144,144]{1,2,0:T(8,128)(4,1)S(1)} %compare_and_fusion, bf16[16,144,1,16,32]{1,4,3,0,2:T(8,128)(2,1)} %copy.22, bf16[16,144,1,16,32]{1,4,3,0,2:T(8,128)(2,1)} %copy.21), kind=kOutput, calls=%fused_computation.116 | convolution fusion | flops 360972416 | bytes 26431488 | tf_op jit(solution)/shard_map/sub | solution.py:57
  255.0 16.4 %convert_bitcast_fusion = bf16[16,144,16,32]{1,3,2,0:T(8,128)(2,1)} fusion(f32[16,16,144,144]{2,3,1,0:T(8,128)} %get-tuple-element.9, f32[16,16,144]{2,1,0:T(8,128)S(1)} %get-tuple-element.8, bf16[16,144,1,16,32]{1,4,3,0,2:T(8,128)(2,1)} %copy.20), kind=kOutput, calls=%fused_computation.58 | convolution fusion | flops 351535104 | bytes 26099712 | tf_op jit(solution)/shard_map/whqk,wkhd->wqhd/dot_general | solution.py:58
  271.4 11.5 %copy.17 = bf16[16,144,16,32]{3,2,0,1:T(8,128)(2,1)} copy(bf16[16,144,16,32]{1,3,2,0:T(8,128)(2,1)} %convert_bitcast_fusion) | data formatting | bytes 4718592 | tf_op jit(solution)/shard_map/convert_element_type | solution.py:61
  282.9 13.0 %reshape.121 = bf16[4,4,2,6,12,512]{5,1,0,4,3,2:T(4,128)(2,1)} reshape(bf16[16,144,16,32]{3,2,0,1:T(8,128)(2,1)} %copy.17) | data formatting | bytes 4718592 | tf_op jit(solution)/shard_map/reshape | solution.py:61
  295.9 3.9 copy.18
  299.8 2.1 reshape_reshape.7
  301.9 3.2 convolution_convert_fusion.1
  305.1 0.1 slice.71
  305.2 0.1 collective-permute-start.4
  305.3 7.7 %collective-permute-done.4 = bf16[2,24,6,512]{3,2,1,0:T(8,128)(2,1)S(1)} collective-permute-done((bf16[2,24,6,512]{3,2,1,0:T(8,128)(2,1)S(1)}, bf16[2,24,6,512]{3,2,1,0:T(8,128)(2,1)S(1)}, u32[]{:S(2)}, u32[]{:S(2)}) %collective-permute-start.4) | collective-permute-done | bytes 294944 | tf_op jit(solution)/shard_map/ppermute | solution.py:18
  313.0 0.1 pad_maximum_fusion.3
  313.2 2.8 pad_maximum_fusion.1
  316.0 7.3 %collective-permute-done.5 = bf16[2,3,48,512]{3,2,1,0:T(8,128)(2,1)S(1)} collective-permute-done((bf16[2,3,48,512]{3,2,1,0:T(8,128)(2,1)S(1)}, bf16[2,3,48,512]{3,2,1,0:T(8,128)(2,1)S(1)}, u32[]{:S(2)}, u32[]{:S(2)}) %collective-permute-start.5) | collective-permute-done | bytes 294944 | tf_op jit(solution)/shard_map/ppermute | solution.py:18
  323.3 0.7 convert_reduce_fusion
  324.0 2.7 fusion.23
  326.8 1.9 maximum_convert_fusion
  328.7 2.2 fusion.24
  331.0 47.1 %fusion.110 = bf16[2304,2048]{1,0:T(8,128)(2,1)} fusion(bf16[512,2048]{0,1:T(8,128)(2,1)} %all-gather.6.cloned.1.call-done, bf16[2304,512]{1,0:T(8,128)(2,1)} %fusion.24, f32[512]{0:T(512)S(1)} %copy-done.9, f32[2304]{0:T(1024)S(1)} %rsqrt.21, f32[2304]{0:T(1024)S(1)} %div.27), kind=kOutput, calls=%fused_computation.8.clone.clone.1 | convolution fusion | flops 5144444928 | bytes 13914112 | tf_op jit(solution)/shard_map/dot_general | solution.py:109
  378.0 8.5 %fusion.18 = f32[2304,512]{1,0:T(8,128)S(1)} fusion(bf16[2048,512]{0,1:T(8,128)(2,1)} %all-gather.8.cloned.1.call-done, bf16[2304,2048]{1,0:T(8,128)(2,1)} %fusion.110), kind=kOutput, calls=%fused_computation.30 | convolution fusion | flops 4831838208 | bytes 16252928 | tf_op jit(solution)/shard_map/dot_general | solution.py:115
  386.5 2.5 add_convert_fusion
  (47 shorter events, 0.7 us)
Async XLA Ops:
  6.5 5.6 %copy-start = (bf16[1,2,24,48,512]{4,3,2,1,0:T(8,128)(2,1)S(1)}, bf16[1,2,24,48,512]{4,3,2,1,0:T(8,128)(2,1)}, u32[]{:S(2)}) copy-start(bf16[1,2,24,48,512]{4,3,2,1,0:T(8,128)(2,1)} %param.8) | copy-start | bytes 7077892
  6.5 5.6 %copy-start.8 = (f32[512]{0:T(512)S(1)}, f32[512]{0:T(512)}, u32[]{:S(2)}) copy-start(f32[512]{0:T(512)} %param.10) | copy-start | bytes 6148
  6.5 104.4 %all-gather.4.cloned.1.call-start = ((), (), s32[]{:S(2)}) async-start(), calls=%async_computation | async-start | bytes 1622016 | tf_op jit(solution)/shard_map/all_gather | solution.py:86
  7.3 12.4 %copy-start.7 = (s32[24,48]{1,0:T(8,128)S(1)}, s32[24,48]{1,0:T(8,128)}, u32[]{:S(2)}) copy-start(s32[24,48]{1,0:T(8,128)} %param.9) | copy-start | bytes 13828
  7.3 13.0 %copy-start.6 = (bf16[512,16]{0,1:T(8,128)(2,1)S(1)}, bf16[512,16]{0,1:T(8,128)(2,1)}, u32[]{:S(2)}) copy-start(bf16[512,16]{0,1:T(8,128)(2,1)} %param.12) | copy-start | bytes 49156
  7.3 323.7 %all-gather.6.cloned.1.call-start = ((), (), s32[]{:S(2)}) async-start(), calls=%async_computation.1 | async-start | bytes 2162688 | tf_op jit(solution)/shard_map/all_gather | solution.py:111
  13.1 1.4 copy-start.5
  14.5 88.2 %collective-permute-start = (bf16[2,3,48,512]{3,2,1,0:T(8,128)(2,1)S(1)}, bf16[2,3,48,512]{3,2,1,0:T(8,128)(2,1)S(1)}, u32[]{:S(2)}, u32[]{:S(2)}) collective-permute-start(bf16[2,3,48,512]{3,2,1,0:T(8,128)(2,1)S(1)} %slice.61), channel_id=1, source_target_pairs={{2,0},{4,2},{6,4},{0,6},{3,1},{5,3},{7,5},{1,7},{10,8},{12,10},{14... | collective-permute-start | bytes 884744 | tf_op jit(solution)/shard_map/ppermute | solution.py:18
  19.7 78.8 %collective-permute-start.2 = (bf16[3,48]{1,0:T(4,128)(2,1)S(1)}, bf16[3,48]{1,0:T(4,128)(2,1)S(1)}, u32[]{:S(2)}, u32[]{:S(2)}) collective-permute-start(bf16[3,48]{1,0:T(4,128)(2,1)S(1)} %slice.66), channel_id=1, source_target_pairs={{2,0},{4,2},{6,4},{0,6},{3,1},{5,3},{7,5},{1,7},{10,8},{12,10},{14... | collective-permute-start | bytes 872 | tf_op jit(solution)/shard_map/ppermute | solution.py:18
  20.2 357.8 %all-gather.8.cloned.1.call-start = ((), (), s32[]{:S(2)}) async-start(), calls=%async_computation.2 | async-start | bytes 2162688 | tf_op jit(solution)/shard_map/all_gather | solution.py:117
  98.5 3.9 collective-permute-start.3
  102.8 7.8 %collective-permute-start.1 = (bf16[2,24,6,512]{3,2,1,0:T(8,128)(2,1)S(1)}, bf16[2,24,6,512]{3,2,1,0:T(8,128)(2,1)S(1)}, u32[]{:S(2)}, u32[]{:S(2)}) collective-permute-start(bf16[2,24,6,512]{3,2,1,0:T(8,128)(2,1)S(1)} %pad_maximum_fusion.2), channel_id=1, source_target_pairs={{1,0},{0,1},{3,2},{2,3},{5,4},{4,5},{7,6},{6,7},{9,8},{8,9},{11,10... | collective-permute-start | bytes 884744 | tf_op jit(solution)/shard_map/ppermute | solution.py:18
  305.0 8.0 %copy-start.4 = (bf16[2304,512]{1,0:T(8,128)(2,1)}, bf16[2304,512]{1,0:T(8,128)(2,1)S(1)}, u32[]{:S(2)}) copy-start(bf16[2304,512]{1,0:T(8,128)(2,1)S(1)} %convolution_convert_fusion.1) | copy-start | bytes 7077892
  305.1 18.2 %copy-start.1 = (bf16[1,2,24,48,512]{4,3,2,1,0:T(8,128)(2,1)S(1)}, bf16[1,2,24,48,512]{4,3,2,1,0:T(8,128)(2,1)}, u32[]{:S(2)}) copy-start(bf16[1,2,24,48,512]{4,3,2,1,0:T(8,128)(2,1)} %param.8) | copy-start | bytes 7077892
  305.2 7.8 %collective-permute-start.4 = (bf16[2,24,6,512]{3,2,1,0:T(8,128)(2,1)S(1)}, bf16[2,24,6,512]{3,2,1,0:T(8,128)(2,1)S(1)}, u32[]{:S(2)}, u32[]{:S(2)}) collective-permute-start(bf16[2,24,6,512]{3,2,1,0:T(8,128)(2,1)S(1)} %slice.71), channel_id=1, source_target_pairs={{1,0},{0,1},{3,2},{2,3},{5,4},{4,5},{7,6},{6,7},{9,8},{8,9},{11,10... | collective-permute-start | bytes 884744 | tf_op jit(solution)/shard_map/ppermute | solution.py:18
  313.1 10.2 %collective-permute-start.5 = (bf16[2,3,48,512]{3,2,1,0:T(8,128)(2,1)S(1)}, bf16[2,3,48,512]{3,2,1,0:T(8,128)(2,1)S(1)}, u32[]{:S(2)}, u32[]{:S(2)}) collective-permute-start(bf16[2,3,48,512]{3,2,1,0:T(8,128)(2,1)S(1)} %pad_maximum_fusion.3), channel_id=1, source_target_pairs={{6,0},{0,2},{2,4},{4,6},{7,1},{1,3},{3,5},{5,7},{14,8},{8,10},{10,... | collective-permute-start | bytes 884744 | tf_op jit(solution)/shard_map/ppermute | solution.py:18
  316.0 7.3 %copy-start.2 = (bf16[2,21,48,512]{3,2,1,0:T(8,128)(2,1)}, bf16[2,21,48,512]{3,2,1,0:T(8,128)(2,1)S(1)}, u32[]{:S(2)}) copy-start(bf16[2,21,48,512]{3,2,1,0:T(8,128)(2,1)S(1)} %pad_maximum_fusion.1) | copy-start | bytes 6193156
  328.7 2.3 copy-start.9
  378.0 8.5 %copy-start.3 = (bf16[2,21,48,512]{3,2,1,0:T(8,128)(2,1)S(1)}, bf16[2,21,48,512]{3,2,1,0:T(8,128)(2,1)}, u32[]{:S(2)}) copy-start(bf16[2,21,48,512]{3,2,1,0:T(8,128)(2,1)} %copy-done.2) | copy-start | bytes 6193156
Sparse Core Ops, SparseCore 0:
  10.3 60.3 all-gather.3
  73.7 56.7 all-gather.5
  313.3 57.8 all-gather.7
where the time goes:
time: 402 us; the launch traced here: 396 us
  local copies, waits for them, and re-layouts  151 us (38%)
  matrix products  102 us (25%)
  blocking collectives  76.2 us (19%)
  waiting for transfers between devices  25.3 us (6%)
  other arithmetic  21.1 us (5%)
  between operations  13.7 us (3%)
  starting transfers between devices  6.03 us (2%)
    all_gather x1, blocking collectives, body(): lax.all_gather(w_proj, ('mem', 'lat', 'lon'), axis=1, tiled=True)  76.2 us
    dot_general x1, matrix products, body(): jnp.dot(normed2, lax.all_gather(w_up, ('mem', 'lat', 'lon'), axis=1, tile...  47.1 us
    unnamed x23, local copies, waits for them, and re-layouts  38.4 us
    reshape x1, local copies, waits for them, and re-layouts, attend(): windowed.transpose(1, 3, 0, 2, 4, 5)  32.5 us
    ppermute x6, waiting for transfers between devices, shifted_2(): return lax.ppermute(block, axis, route)  24.5 us
    slice x1, local copies, waits for them, and re-layouts, attend(): windowed[:, :, 2]  24 us
    sub x1, matrix products, attend(): attn_probs = jax.nn.softmax(scores, axis=-1).astype(jnp.bfloat16)  19.9 us
    dot_general x1, matrix products, attend(): jnp.einsum('whqk,wkhd->wqhd', attn_probs, windowed[:, :, 2], preferred_el...  16.4 us
  transfers between devices with their start and end apart: 9, of which 4 were waited for; matrix products, arithmetic and copies ran while one was open for 66% of the time, Pallas kernels for 0%

commit v1 on v0

--- a/solution.py
+++ b/solution.py
@@ -10,6 +10,29 @@
 SH = 3
 SL = 6
 eps = 1e-05
+
+
+def laid_out(pieces, dim):
+    shape = list(pieces.shape[1:])
+    shape[dim] *= pieces.shape[0]
+    return jnp.moveaxis(pieces, 0, dim).reshape(shape)
+
+
+def collected_by_bits(x, axis):
+    length, index = (lax.axis_size(axis), lax.axis_index(axis))
+    blocks, apart = (x[None], 1)
+    while apart < length:
+        received = lax.ppermute(blocks, axis, [(i, i ^ apart) for i in range(length)])
+        low = index & apart == 0
+        blocks = jnp.concatenate(
+            [jnp.where(low, blocks, received), jnp.where(low, received, blocks)]
+        )
+        apart *= 2
+    return blocks
+
+
+def collect(value, axis, dim):
+    return laid_out(collected_by_bits(value, axis), dim)
 
 
 def shifted_2(block, axis, distance):
@@ -94,7 +117,7 @@
     attn_out = (
         jnp.dot(
             proj_tok_rows,
-            lax.all_gather(w_proj, ("mem", "lat", "lon"), axis=1, tiled=True),
+            collect(w_proj, ("mem", "lat", "lon"), 1),
             preferred_element_type=jnp.float32,
         )
         .astype(jnp.bfloat16)

time: 402 us -> 365 us (0.908)
  blocking collectives: 76.2 us -> 0 us
  waiting for transfers between devices: 25.3 us -> 53.5 us
  starting transfers between devices: 6.03 us -> 16 us
    all_gather x1 -> x0, blocking collectives: 76.2 us -> none  [body(): lax.all_gather(w_proj, ('mem', 'lat', 'lon'), axis=1, tiled=True)]
    all_gather x1, waiting for transfers between devices: 0.02 us -> 17.7 us  [body(): lax.all_gather(w_qkv, ('mem', 'lat', 'lon'), axis=1, tiled=True)]
    ppermute x0 -> x5, waiting for transfers between devices: none -> 7.73 us  [collected_by_bits(): lax.ppermute(blocks, axis, [(i, i ^ apart) for i in range(length)])]
    ppermute x0 -> x5, starting transfers between devices: none -> 7.72 us  [collected_by_bits(): lax.ppermute(blocks, axis, [(i, i ^ apart) for i in range(length)])]
  transfers between devices with their start and end apart: 9 -> 14, of which waited for: 4 -> 9; matrix products, arithmetic and copies ran while one was open for 66% -> 73% of each run, Pallas kernels for 0% -> 0%
where the time goes in v1:
time: 365 us; the launch traced here: 359 us
  local copies, waits for them, and re-layouts  151 us (41%)
  matrix products  102 us (28%)
  waiting for transfers between devices  53.5 us (15%)
  other arithmetic  22.1 us (6%)
  starting transfers between devices  16 us (4%)
  between operations  13.7 us (4%)
    dot_general x1, matrix products, body(): jnp.dot(normed2, lax.all_gather(w_up, ('mem', 'lat', 'lon'), axis=1, tile...  47.1 us
    unnamed x23, local copies, waits for them, and re-layouts  38.4 us
    reshape x1, local copies, waits for them, and re-layouts, attend(): windowed.transpose(1, 3, 0, 2, 4, 5)  32.5 us
    ppermute x6, waiting for transfers between devices, shifted_2(): return lax.ppermute(block, axis, route)  27.3 us
    slice x1, local copies, waits for them, and re-layouts, attend(): windowed[:, :, 2]  24 us
    sub x1, matrix products, attend(): attn_probs = jax.nn.softmax(scores, axis=-1).astype(jnp.bfloat16)  19.9 us
    all_gather x1, waiting for transfers between devices, body(): lax.all_gather(w_qkv, ('mem', 'lat', 'lon'), axis=1, tiled=True)  17.7 us
    dot_general x1, matrix products, attend(): jnp.einsum('whqk,wkhd->wqhd', attn_probs, windowed[:, :, 2], preferred_el...  16.5 us
  transfers between devices with their start and end apart: 14, of which 9 were waited for; matrix products, arithmetic and copies ran while one was open for 73% of the time, Pallas kernels for 0%

profile of v1, /device:TPU:0, one launch (start us, length us, event | category | flops | bytes accessed | tf_op | source)
XLA Modules:
  0.0 358.8 jit_solution(15074551082594106125)
XLA Ops:
  6.5 0.7 all-gather.4.cloned.1.call-update
  7.3 3.0 collective-permute-start.4
  10.3 2.0 convert_reduce_fusion.1
  12.4 2.7 fusion.27
  15.2 0.9 fusion.29
  16.1 1.4 copy-done.5
  17.5 3.7 %collective-permute-start = (bf16[2,3,48,512]{3,2,1,0:T(8,128)(2,1)S(1)}, bf16[2,3,48,512]{3,2,1,0:T(8,128)(2,1)S(1)}, u32[]{:S(2)}, u32[]{:S(2)}) collective-permute-start(bf16[2,3,48,512]{3,2,1,0:T(8,128)(2,1)S(1)} %slice.61), channel_id=1, source_target_pairs={{2,0},{4,2},{6,4},{0,6},{3,1},{5,3},{7,5},{1,7},{10,8},{12,10},{14... | collective-permute-start | bytes 884744 | tf_op jit(solution)/shard_map/ppermute | solution.py:41
  21.2 0.5 collective-permute-start.2
  21.8 1.7 slice.60
  23.8 4.5 %collective-permute-done.2 = bf16[3,48]{1,0:T(4,128)(2,1)S(1)} collective-permute-done((bf16[3,48]{1,0:T(4,128)(2,1)S(1)}, bf16[3,48]{1,0:T(4,128)(2,1)S(1)}, u32[]{:S(2)}, u32[]{:S(2)}) %collective-permute-start.2) | collective-permute-done | bytes 320 | tf_op jit(solution)/shard_map/ppermute | solution.py:41
  28.7 3.3 collective-permute-done.3
  32.6 2.9 collective-permute-start.6
  35.5 2.2 collective-permute-done.6
  37.9 1.4 compare_and_fusion
  39.4 1.6 collective-permute-start.8
  41.0 2.1 collective-permute-start.1
  43.0 0.6 slice_maximum_fusion
  43.6 5.1 %collective-permute-done.8 = bf16[16,512,16]{1,2,0:T(8,128)(2,1)S(1)} collective-permute-done((bf16[16,512,16]{1,2,0:T(8,128)(2,1)S(1)}, bf16[16,512,16]{1,2,0:T(8,128)(2,1)S(1)}, u32[]{:S(2)}, u32[]{:S(2)}) %collective-permute-start.8) | collective-permute-done | bytes 262176 | tf_op jit(solution)/shard_map/ppermute | solution.py:25
  48.8 0.8 pad_maximum_fusion.2
  49.6 2.9 collective-permute-done.1
  52.8 17.7 %all-gather.4.cloned.1.call-done = bf16[512,1536]{0,1:T(8,128)(2,1)} async-done(((bf16[512,48]{0,1:T(8,128)(2,1)}), bf16[512,1536]{0,1:T(8,128)(2,1)}) %all-gather.4.cloned.1.call-update) | async-done | bytes 1572880 | tf_op jit(solution)/shard_map/all_gather | solution.py:109
  70.5 7.2 %convolution_convert_fusion = bf16[2304,1536]{1,0:T(8,128)(2,1)} fusion(bf16[2304,512]{1,0:T(8,128)(2,1)S(1)} %bitcast.97, bf16[512,1536]{0,1:T(8,128)(2,1)} %all-gather.4.cloned.1.call-done), kind=kOutput, calls=%fused_computation.29 | convolution fusion | flops 3627417600 | bytes 11010048 | tf_op jit(solution)/shard_map/dot_general | solution.py:107
  77.8 11.3 %reshape_reshape.6 = bf16[2,4,6,4,12,1536]{5,4,3,2,1,0:T(8,128)(2,1)} reshape(bf16[2304,1536]{1,0:T(8,128)(2,1)} %convolution_convert_fusion) | data formatting | bytes 14155776 | tf_op jit(solution)/shard_map/reshape;reshape | solution.py:58
  89.1 12.0 %copy.11 = bf16[4,4,2,6,12,1536]{5,1,0,4,3,2:T(4,128)(2,1)} copy(bf16[4,4,2,6,12,1536]{5,4,1,3,0,2:T(8,128)(2,1)} %bitcast.90) | data formatting | bytes 14155776 | tf_op jit(solution)/shard_map/transpose | solution.py:59
  101.1 32.5 %reshape.123 = bf16[16,144,3,16,32]{4,3,2,0,1:T(8,128)(2,1)} reshape(bf16[4,4,2,6,12,1536]{5,1,0,4,3,2:T(4,128)(2,1)} %copy.11) | data formatting | bytes 14155776 | tf_op jit(solution)/shard_map/reshape | solution.py:59
  133.6 24.0 %fusion.88 = (bf16[16,144,1,16,32]{4,3,2,0,1:T(8,128)(2,1)}, bf16[16,144,1,16,32]{4,3,2,0,1:T(8,128)(2,1)}, bf16[16,144,1,16,32]{4,3,2,0,1:T(8,128)(2,1)}) fusion(bf16[16,144,3,16,32]{4,3,2,0,1:T(8,128)(2,1)} %reshape.123), kind=kLoop, calls=%fused_computation.130 | loop fusion | bytes 14155776 | tf_op jit(solution)/shard_map/slice | solution.py:82
  157.6 12.3 %copy.21 = bf16[16,144,1,16,32]{1,4,3,0,2:T(8,128)(2,1)} copy(bf16[16,144,1,16,32]{4,3,2,0,1:T(8,128)(2,1)} %get-tuple-element.6) | data formatting | bytes 4718592
  169.9 12.4 %copy.22 = bf16[16,144,1,16,32]{1,4,3,0,2:T(8,128)(2,1)} copy(bf16[16,144,1,16,32]{4,3,2,0,1:T(8,128)(2,1)} %get-tuple-element.7) | data formatting | bytes 4718592
  182.3 12.3 %copy.20 = bf16[16,144,1,16,32]{1,4,3,0,2:T(8,128)(2,1)} copy(bf16[16,144,1,16,32]{4,3,2,0,1:T(8,128)(2,1)} %get-tuple-element.5) | data formatting | bytes 4718592
  194.6 19.9 %fusion.89 = (f32[16,16,144]{2,1,0:T(8,128)S(1)}, f32[16,16,144,144]{2,3,1,0:T(8,128)}) fusion(pred[16,144,144]{1,2,0:T(8,128)(4,1)S(1)} %compare_and_fusion, bf16[16,144,1,16,32]{1,4,3,0,2:T(8,128)(2,1)} %copy.22, bf16[16,144,1,16,32]{1,4,3,0,2:T(8,128)(2,1)} %copy.21), kind=kOutput, calls=%fused_computation.131 | convolution fusion | flops 360972416 | bytes 26431488 | tf_op jit(solution)/shard_map/sub | solution.py:80
  214.5 16.5 %convert_bitcast_fusion = bf16[16,144,16,32]{1,3,2,0:T(8,128)(2,1)} fusion(f32[16,16,144,144]{2,3,1,0:T(8,128)} %get-tuple-element.19, f32[16,16,144]{2,1,0:T(8,128)S(1)} %get-tuple-element.18, bf16[16,144,1,16,32]{1,4,3,0,2:T(8,128)(2,1)} %copy.20), kind=kOutput, calls=%fused_computation.58 | convolution fusion | flops 351535104 | bytes 26099712 | tf_op jit(solution)/shard_map/whqk,wkhd->wqhd/dot_general | solution.py:81
  231.0 11.5 %copy.17 = bf16[16,144,16,32]{3,2,0,1:T(8,128)(2,1)} copy(bf16[16,144,16,32]{1,3,2,0:T(8,128)(2,1)} %convert_bitcast_fusion) | data formatting | bytes 4718592 | tf_op jit(solution)/shard_map/convert_element_type | solution.py:84
  242.5 13.0 %reshape.124 = bf16[4,4,2,6,12,512]{5,1,0,4,3,2:T(4,128)(2,1)} reshape(bf16[16,144,16,32]{3,2,0,1:T(8,128)(2,1)} %copy.17) | data formatting | bytes 4718592 | tf_op jit(solution)/shard_map/reshape | solution.py:84
  255.4 3.9 %copy.18 = bf16[2,4,6,4,12,512]{5,4,3,2,1,0:T(8,128)(2,1)S(1)} copy(bf16[2,4,6,4,12,512]{5,3,1,4,2,0:T(4,128)(2,1)} %bitcast.94) | data formatting | bytes 4718592 | tf_op jit(solution)/shard_map/transpose | solution.py:87
  259.3 2.1 reshape_reshape.7
  261.4 3.2 convolution_convert_fusion.1
  264.7 1.5 collective-permute-start.9
  266.2 9.8 %collective-permute-done.9 = bf16[2,24,6,512]{3,2,1,0:T(8,128)(2,1)S(1)} collective-permute-done((bf16[2,24,6,512]{3,2,1,0:T(8,128)(2,1)S(1)}, bf16[2,24,6,512]{3,2,1,0:T(8,128)(2,1)S(1)}, u32[]{:S(2)}, u32[]{:S(2)}) %collective-permute-start.9) | collective-permute-done | bytes 294944 | tf_op jit(solution)/shard_map/ppermute | solution.py:41
  276.1 0.5 collective-permute-start.10
  276.6 2.8 pad_maximum_fusion.1
  279.4 6.8 %collective-permute-done.10 = bf16[2,3,48,512]{3,2,1,0:T(8,128)(2,1)S(1)} collective-permute-done((bf16[2,3,48,512]{3,2,1,0:T(8,128)(2,1)S(1)}, bf16[2,3,48,512]{3,2,1,0:T(8,128)(2,1)S(1)}, u32[]{:S(2)}, u32[]{:S(2)}) %collective-permute-start.10) | collective-permute-done | bytes 294944 | tf_op jit(solution)/shard_map/ppermute | solution.py:41
  286.2 0.7 convert_reduce_fusion
  287.0 2.7 fusion.23
  289.8 1.9 maximum_convert_fusion
  291.7 2.2 fusion.24
  293.9 47.1 %fusion.110 = bf16[2304,2048]{1,0:T(8,128)(2,1)} fusion(bf16[512,2048]{0,1:T(8,128)(2,1)} %all-gather.6.cloned.1.call-done, bf16[2304,512]{1,0:T(8,128)(2,1)} %fusion.24, f32[512]{0:T(512)S(1)} %copy-done.9, f32[2304]{0:T(1024)S(1)} %rsqrt.21, f32[2304]{0:T(1024)S(1)} %div.27), kind=kOutput, calls=%fused_computation.8.clone.clone.1 | convolution fusion | flops 5144444928 | bytes 13914112 | tf_op jit(solution)/shard_map/dot_general | solution.py:132
  341.0 8.5 %fusion.18 = f32[2304,512]{1,0:T(8,128)S(1)} fusion(bf16[2048,512]{0,1:T(8,128)(2,1)} %all-gather.8.cloned.1.call-done, bf16[2304,2048]{1,0:T(8,128)(2,1)} %fusion.110), kind=kOutput, calls=%fused_computation.30 | convolution fusion | flops 4831838208 | bytes 16252928 | tf_op jit(solution)/shard_map/dot_general | solution.py:138
  349.5 2.5 add_convert_fusion
  (66 shorter events, 2.4 us)
Async XLA Ops:
  6.5 8.6 %copy-start = (bf16[1,2,24,48,512]{4,3,2,1,0:T(8,128)(2,1)S(1)}, bf16[1,2,24,48,512]{4,3,2,1,0:T(8,128)(2,1)}, u32[]{:S(2)}) copy-start(bf16[1,2,24,48,512]{4,3,2,1,0:T(8,128)(2,1)} %param.8) | copy-start | bytes 7077892
  6.5 8.6 %copy-start.8 = (f32[512]{0:T(512)S(1)}, f32[512]{0:T(512)}, u32[]{:S(2)}) copy-start(f32[512]{0:T(512)} %param.10) | copy-start | bytes 6148
  6.5 64.0 %all-gather.4.cloned.1.call-start = ((), (), s32[]{:S(2)}) async-start(), calls=%async_computation | async-start | bytes 1622016 | tf_op jit(solution)/shard_map/all_gather | solution.py:109
  7.3 286.7 %all-gather.6.cloned.1.call-start = ((), (), s32[]{:S(2)}) async-start(), calls=%async_computation.1 | async-start | bytes 2162688 | tf_op jit(solution)/shard_map/all_gather | solution.py:134
  7.3 13.9 %copy-start.7 = (s32[24,48]{1,0:T(8,128)S(1)}, s32[24,48]{1,0:T(8,128)}, u32[]{:S(2)}) copy-start(s32[24,48]{1,0:T(8,128)} %param.9) | copy-start | bytes 13828
  7.3 21.1 %collective-permute-start.4 = (bf16[1,512,16]{1,2,0:T(8,128)(2,1)}, bf16[1,512,16]{1,2,0:T(8,128)(2,1)S(1)}, u32[]{:S(2)}, u32[]{:S(2)}) collective-permute-start(bf16[1,512,16]{1,2,0:T(8,128)(2,1)} %bitcast.99), channel_id=1, source_target_pairs={{0,1},{1,0},{2,3},{3,2},{4,5},{5,4},{6,7},{7,6},{8,9},{9,8},{10,11... | collective-permute-start | bytes 49160 | tf_op jit(solution)/shard_map/ppermute | solution.py:25
  15.1 13.3 %copy-start.6 = (bf16[512,16]{0,1:T(8,128)(2,1)S(1)}, bf16[512,16]{0,1:T(8,128)(2,1)}, u32[]{:S(2)}) copy-start(bf16[512,16]{0,1:T(8,128)(2,1)} %param.12) | copy-start | bytes 49156
  16.1 1.4 copy-start.5
  17.5 23.4 %collective-permute-start = (bf16[2,3,48,512]{3,2,1,0:T(8,128)(2,1)S(1)}, bf16[2,3,48,512]{3,2,1,0:T(8,128)(2,1)S(1)}, u32[]{:S(2)}, u32[]{:S(2)}) collective-permute-start(bf16[2,3,48,512]{3,2,1,0:T(8,128)(2,1)S(1)} %slice.61), channel_id=1, source_target_pairs={{2,0},{4,2},{6,4},{0,6},{3,1},{5,3},{7,5},{1,7},{10,8},{12,10},{14... | collective-permute-start | bytes 884744 | tf_op jit(solution)/shard_map/ppermute | solution.py:41
  21.2 7.1 %collective-permute-start.2 = (bf16[3,48]{1,0:T(4,128)(2,1)S(1)}, bf16[3,48]{1,0:T(4,128)(2,1)S(1)}, u32[]{:S(2)}, u32[]{:S(2)}) collective-permute-start(bf16[3,48]{1,0:T(4,128)(2,1)S(1)} %slice.66), channel_id=1, source_target_pairs={{2,0},{4,2},{6,4},{0,6},{3,1},{5,3},{7,5},{1,7},{10,8},{12,10},{14... | collective-permute-start | bytes 872 | tf_op jit(solution)/shard_map/ppermute | solution.py:41
  21.7 319.2 %all-gather.8.cloned.1.call-start = ((), (), s32[]{:S(2)}) async-start(), calls=%async_computation.2 | async-start | bytes 2162688 | tf_op jit(solution)/shard_map/all_gather | solution.py:140
  28.3 3.7 %collective-permute-start.3 = (bf16[24,6]{1,0:T(8,128)(2,1)S(1)}, bf16[24,6]{1,0:T(8,128)(2,1)S(1)}, u32[]{:S(2)}, u32[]{:S(2)}) collective-permute-start(bf16[24,6]{1,0:T(8,128)(2,1)S(1)} %pad_maximum_fusion.9), channel_id=1, source_target_pairs={{1,0},{0,1},{3,2},{2,3},{5,4},{4,5},{7,6},{6,7},{9,8},{8,9},{11,10... | collective-permute-start | bytes 872 | tf_op jit(solution)/shard_map/ppermute | solution.py:41
  28.5 4.0 %collective-permute-start.5 = (bf16[2,512,16]{1,2,0:T(8,128)(2,1)S(1)}, bf16[2,512,16]{1,2,0:T(8,128)(2,1)S(1)}, u32[]{:S(2)}, u32[]{:S(2)}) collective-permute-start(bf16[2,512,16]{1,2,0:T(8,128)(2,1)S(1)} %pad_maximum_fusion.8), channel_id=1, source_target_pairs={{0,2},{1,3},{2,0},{3,1},{4,6},{5,7},{6,4},{7,5},{8,10},{9,11},{10,... | collective-permute-start | bytes 98312 | tf_op jit(solution)/shard_map/ppermute | solution.py:25
  32.6 5.2 %collective-permute-start.6 = (bf16[4,512,16]{1,2,0:T(8,128)(2,1)S(1)}, bf16[4,512,16]{1,2,0:T(8,128)(2,1)S(1)}, u32[]{:S(2)}, u32[]{:S(2)}) collective-permute-start(bf16[4,512,16]{1,2,0:T(8,128)(2,1)S(1)} %pad_maximum_fusion.7), channel_id=1, source_target_pairs={{0,4},{1,5},{2,6},{3,7},{4,0},{5,1},{6,2},{7,3},{8,12},{9,13},{10,... | collective-permute-start | bytes 196616 | tf_op jit(solution)/shard_map/ppermute | solution.py:25
  37.8 1.5 collective-permute-start.7
  39.4 9.4 %collective-permute-start.8 = (bf16[16,512,16]{1,2,0:T(8,128)(2,1)S(1)}, bf16[16,512,16]{1,2,0:T(8,128)(2,1)S(1)}, u32[]{:S(2)}, u32[]{:S(2)}) collective-permute-start(bf16[16,512,16]{1,2,0:T(8,128)(2,1)S(1)} %pad_maximum_fusion.5), channel_id=1, source_target_pairs={{0,16},{1,17},{2,18},{3,19},{4,20},{5,21},{6,22},{7,23},{8,24},{9,... | collective-permute-start | bytes 786440 | tf_op jit(solution)/shard_map/ppermute | solution.py:25
  41.0 11.5 %collective-permute-start.1 = (bf16[2,24,6,512]{3,2,1,0:T(8,128)(2,1)S(1)}, bf16[2,24,6,512]{3,2,1,0:T(8,128)(2,1)S(1)}, u32[]{:S(2)}, u32[]{:S(2)}) collective-permute-start(bf16[2,24,6,512]{3,2,1,0:T(8,128)(2,1)S(1)} %pad_maximum_fusion.3), channel_id=1, source_target_pairs={{1,0},{0,1},{3,2},{2,3},{5,4},{4,5},{7,6},{6,7},{9,8},{8,9},{11,10... | collective-permute-start | bytes 884744 | tf_op jit(solution)/shard_map/ppermute | solution.py:41
  264.6 11.4 %copy-start.4 = (bf16[2304,512]{1,0:T(8,128)(2,1)}, bf16[2304,512]{1,0:T(8,128)(2,1)S(1)}, u32[]{:S(2)}) copy-start(bf16[2304,512]{1,0:T(8,128)(2,1)S(1)} %convolution_convert_fusion.1) | copy-start | bytes 7077892
  264.6 21.6 %copy-start.1 = (bf16[1,2,24,48,512]{4,3,2,1,0:T(8,128)(2,1)S(1)}, bf16[1,2,24,48,512]{4,3,2,1,0:T(8,128)(2,1)}, u32[]{:S(2)}) copy-start(bf16[1,2,24,48,512]{4,3,2,1,0:T(8,128)(2,1)} %param.8) | copy-start | bytes 7077892
  264.7 11.3 %collective-permute-start.9 = (bf16[2,24,6,512]{3,2,1,0:T(8,128)(2,1)S(1)}, bf16[2,24,6,512]{3,2,1,0:T(8,128)(2,1)S(1)}, u32[]{:S(2)}, u32[]{:S(2)}) collective-permute-start(bf16[2,24,6,512]{3,2,1,0:T(8,128)(2,1)S(1)} %slice.71), channel_id=1, source_target_pairs={{1,0},{0,1},{3,2},{2,3},{5,4},{4,5},{7,6},{6,7},{9,8},{8,9},{11,10... | collective-permute-start | bytes 884744 | tf_op jit(solution)/shard_map/ppermute | solution.py:41
  276.1 10.1 %collective-permute-start.10 = (bf16[2,3,48,512]{3,2,1,0:T(8,128)(2,1)S(1)}, bf16[2,3,48,512]{3,2,1,0:T(8,128)(2,1)S(1)}, u32[]{:S(2)}, u32[]{:S(2)}) collective-permute-start(bf16[2,3,48,512]{3,2,1,0:T(8,128)(2,1)S(1)} %pad_maximum_fusion.4), channel_id=1, source_target_pairs={{6,0},{0,2},{2,4},{4,6},{7,1},{1,3},{3,5},{5,7},{14,8},{8,10},{10,... | collective-permute-start | bytes 884744 | tf_op jit(solution)/shard_map/ppermute | solution.py:41
  279.4 6.9 %copy-start.2 = (bf16[2,21,48,512]{3,2,1,0:T(8,128)(2,1)}, bf16[2,21,48,512]{3,2,1,0:T(8,128)(2,1)S(1)}, u32[]{:S(2)}) copy-start(bf16[2,21,48,512]{3,2,1,0:T(8,128)(2,1)S(1)} %pad_maximum_fusion.1) | copy-start | bytes 6193156
  291.7 2.3 copy-start.9
  341.0 8.5 %copy-start.3 = (bf16[2,21,48,512]{3,2,1,0:T(8,128)(2,1)S(1)}, bf16[2,21,48,512]{3,2,1,0:T(8,128)(2,1)}, u32[]{:S(2)}) copy-start(bf16[2,21,48,512]{3,2,1,0:T(8,128)(2,1)} %copy-done.2) | copy-start | bytes 6193156
Sparse Core Ops, SparseCore 0:
  10.3 60.1 all-gather.3
  73.5 55.2 all-gather.5
  276.7 56.4 all-gather.7
